TPU v7x, 32 devices: a whole 2x2x4 slice. The times are simulated.
32 devices in a mesh: fit: 2 (over x), comp: 4 (over z), data: 4 (over y, core).
Axes of the slice: x: 2, y: 2, z: 4, core: 2. Of those that a mesh axis runs over, the one named last changes fastest.
Arguments:
- points: bfloat16 [8192, 256], P(('fit', 'data')), parts along dimension 0
- mu_init: float32 [32768, 256], P(('fit', 'comp')), parts along dimension 0
- logpi_init: float32 [32768], P(('fit', 'comp')), parts along dimension 0
- inv_temp: float32 [3], replicated
Outputs:
- output 1: float32 [32768, 256], P(('fit', 'comp', 'data')), parts along dimension 0
- output 2: float32 [32768], P(('fit', 'comp', 'data')), parts along dimension 0
- output 3: float32 [8192], P(('fit', 'data')), parts along dimension 0
There are 2 independent parts. A program takes and returns all parts, laid end to end along the dimension named above; an argument that names none is the same for every part.
All inputs are finite; a program needn't handle non-finite values.
Results may differ from a plain program's by a relative error of at most 0.00362.
Values are sent between devices in bfloat16 or wider.
A program may use at most 1 GiB of HBM per device.

v0:
```python
import jax
import jax.numpy as jnp
from jax import lax
from jax.sharding import PartitionSpec as P

MEAN_EPS = 1e-6
PRIOR_ALPHA = 1e-3


def solution(mesh):
    n_comp_dev = mesh.shape['comp']
    n_data_dev = mesh.shape['data']

    def local_fit(points, mu_init, logpi_init, inv_temp):
        n_points = points.shape[0] * n_data_dev
        n_total = mu_init.shape[0] * n_comp_dev
        pt_sq = jnp.einsum('nd,nd->n', points, points, preferred_element_type=jnp.float32)
        means = mu_init
        log_wts = logpi_init
        log_norm = pt_sq
        n_sweeps = inv_temp.shape[0]
        for step in range(n_sweeps):
            mu_bf = means.astype(jnp.bfloat16)
            cross_dot = jnp.einsum('nd,kd->nk', points, mu_bf, preferred_element_type=jnp.float32)
            mu_sq = jnp.sum(means * means, axis=1)
            logits = log_wts[None, :] - inv_temp[step] * (pt_sq[:, None] - 2.0 * cross_dot + mu_sq[None, :])
            row_max = lax.pmax(jnp.max(logits, axis=1), 'comp')
            row_sum = lax.psum(jnp.sum(jnp.exp(logits - row_max[:, None]), axis=1), 'comp')
            log_norm = row_max + jnp.log(row_sum)
            respons = jnp.exp(logits - log_norm[:, None])
            count_part = jnp.sum(respons, axis=0)
            stat_part = jnp.einsum('nk,nd->kd', respons.astype(jnp.bfloat16), points, preferred_element_type=jnp.float32)
            if step + 1 < n_sweeps:
                stat_sum, counts = lax.psum((stat_part, count_part), 'data')
            else:
                stat_sum = lax.psum_scatter(stat_part, 'data', scatter_dimension=0, tiled=True)
                counts = lax.psum_scatter(count_part, 'data', scatter_dimension=0, tiled=True)
            means = stat_sum / (counts[:, None] + MEAN_EPS)
            log_wts = jnp.log((counts + PRIOR_ALPHA) / (n_points + n_total * PRIOR_ALPHA))
        return means, log_wts, log_norm

    return jax.shard_map(
        local_fit,
        mesh=mesh,
        in_specs=(P(('fit', 'data'), None), P(('fit', 'comp'), None), P(('fit', 'comp')), P(None)),
        out_specs=(P(('fit', 'comp', 'data'), None), P(('fit', 'comp', 'data')), P(('fit', 'data'))),
        check_vma=False,
    )
```

profile of v0, /device:TPU:1, one launch (start us, length us, event | category | flops | bytes accessed | tf_op | source)
XLA Modules:
  0.0 389.4 jit_solution(5814218458273507625)
XLA Ops:
  7.2 0.0 all-reduce.4.cloned.1.call-start
  7.2 1.3 fusion.18
  8.5 1.4 fusion.19
  9.8 2.8 multiply_reduce_fusion.2
  12.6 0.0 copy-start
  12.6 10.9 %fusion.20 = (f32[1024]{0:T(1024)S(1)}, f32[1024,4096]{1,0:T(8,128)}) fusion(f32[4096]{0:T(1024)S(1)} %multiply_reduce_fusion.2, bf16[1024,256]{1,0:T(8,128)(2,1)} %param.4, f32[4096,256]{1,0:T(8,128)} %param.5, f32[1024]{0:T(1024)S(1)} %fusion.18, f32[]{:T(128)} %bitcast, f32[4096]{0:T(1024)} %param.6), kind=kOutput, calls=%fused_computation.42 | convolution fusion | flops 2173697024 | bytes 21536772 | tf_op jit(solution)/shard_map/nd,kd->nk/dot_general | solution.py:24
  23.5 10.7 %pmax.21 = f32[1024]{0:T(1024)S(1)} all-reduce(f32[1024]{0:T(1024)S(1)} %get-tuple-element.12), channel_id=1, replica_groups=mesh['fit'=2,'comp'=4,'data'=4] {'comp'}, use_global_device_ids=true, to_apply=%region_2.0 | all-reduce | flops 1024 | bytes 8192 | tf_op jit(solution)/shard_map/pmax | solution.py:27
  34.3 8.1 %exponential_reduce_fusion.2 = f32[1024]{0:T(1024)S(1)} fusion(f32[1024,4096]{1,0:T(8,128)} %get-tuple-element.13, f32[1024]{0:T(1024)S(1)} %pmax.21), kind=kLoop, calls=%fused_computation.7 | loop fusion | flops 8387584 | bytes 16785408 | tf_op jit(solution)/shard_map/reduce_sum | solution.py:28
  42.4 6.6 %psum.49 = f32[1024]{0:T(1024)S(1)} all-reduce(f32[1024]{0:T(1024)S(1)} %exponential_reduce_fusion.2), channel_id=1, replica_groups=mesh['fit'=2,'comp'=4,'data'=4] {'comp'}, use_global_device_ids=true, to_apply=%region_4.0 | all-reduce | flops 1024 | bytes 8192 | tf_op jit(solution)/shard_map/psum | solution.py:28
  49.0 0.0 copy-done
  49.0 11.0 %fusion.10 = f32[4096,256]{1,0:T(8,128)} fusion(bf16[1024,256]{1,0:T(8,128)(2,1)S(1)} %copy-done, f32[1024,4096]{1,0:T(8,128)} %get-tuple-element.13, f32[1024]{0:T(1024)S(1)} %log_add_fusion.2), kind=kOutput, calls=%fused_computation.17 | convolution fusion | flops 2155872256 | bytes 21499904 | tf_op jit(solution)/shard_map/nk,nd->kd/dot_general | solution.py:32
  60.0 0.0 all-reduce.4.cloned.1.call-update
  60.1 0.0 all-reduce.6.cloned.1.call-start
  60.1 8.3 %fusion.1 = f32[4096]{0:T(1024)S(1)} fusion(f32[1024,4096]{1,0:T(8,128)} %get-tuple-element.13, f32[1024]{0:T(1024)S(1)} %log_add_fusion.2), kind=kLoop, calls=%fused_computation.10 | loop fusion | flops 8384512 | bytes 16797696 | tf_op jit(solution)/shard_map/reduce_sum | solution.py:31
  68.4 14.7 %psum.50 = f32[4096]{0:T(1024)S(1)} all-reduce(f32[4096]{0:T(1024)S(1)} %fusion.1), channel_id=1, replica_groups=mesh['fit'=2,'comp'=4,'data'=4] {'data'}, use_global_device_ids=true, to_apply=%region_6.0 | all-reduce | flops 4096 | bytes 32768 | tf_op jit(solution)/shard_map/psum | solution.py:34
  83.1 65.8 %all-reduce.4.cloned.1.call-done = f32[4096,256]{1,0:T(8,128)} async-done(((f32[4096,256]{1,0:T(8,128)}), f32[4096,256]{1,0:T(8,128)}) %all-reduce.4.cloned.1.call-update) | async-done | bytes 4194320 | tf_op jit(solution)/shard_map/psum | solution.py:34
  148.9 2.9 multiply_reduce_fusion.1
  151.7 10.7 %fusion.21 = (f32[1024]{0:T(1024)S(1)}, f32[4096,1024]{1,0:T(8,128)}) fusion(f32[4096]{0:T(1024)S(1)} %multiply_reduce_fusion.1, bf16[1024,256]{1,0:T(8,128)(2,1)S(1)} %copy-done, f32[4096,256]{1,0:T(8,128)} %all-reduce.4.cloned.1.call-done, f32[4096]{0:T(1024)S(1)} %get-tuple-element.7, f32[1024]{0:T(1024)S(1)} %fusion.18, f32[]{:T(128)} %bitcast.1, ...), kind=kOutput, calls=%fused_computation.43 | convolution fusion | flops 2174745600 | bytes 21553156 | tf_op jit(solution)/shard_map/nd,kd->nk/dot_general | solution.py:24
  162.4 9.6 %pmax.22 = f32[1024]{0:T(1024)S(1)} all-reduce(f32[1024]{0:T(1024)S(1)} %get-tuple-element.14), channel_id=1, replica_groups=mesh['fit'=2,'comp'=4,'data'=4] {'comp'}, use_global_device_ids=true, to_apply=%region_10.0 | all-reduce | flops 1024 | bytes 8192 | tf_op jit(solution)/shard_map/pmax | solution.py:27
  172.1 8.0 %exponential_reduce_fusion.1 = f32[1024]{0:T(1024)S(1)} fusion(f32[4096,1024]{1,0:T(8,128)} %get-tuple-element.15, f32[1024]{0:T(1024)S(1)} %pmax.22), kind=kLoop, calls=%fused_computation.1 | loop fusion | flops 8387584 | bytes 16785408 | tf_op jit(solution)/shard_map/reduce_sum | solution.py:28
  180.1 6.6 %psum.52 = f32[1024]{0:T(1024)S(1)} all-reduce(f32[1024]{0:T(1024)S(1)} %exponential_reduce_fusion.1), channel_id=1, replica_groups=mesh['fit'=2,'comp'=4,'data'=4] {'comp'}, use_global_device_ids=true, to_apply=%region_12.0 | all-reduce | flops 1024 | bytes 8192 | tf_op jit(solution)/shard_map/psum | solution.py:28
  186.7 10.3 %fusion.8 = f32[4096,256]{1,0:T(8,128)} fusion(bf16[1024,256]{1,0:T(8,128)(2,1)S(1)} %copy-done, f32[4096,1024]{1,0:T(8,128)} %get-tuple-element.15, f32[1024]{0:T(1024)S(1)} %log_add_fusion.1), kind=kOutput, calls=%fused_computation.16 | convolution fusion | flops 2155872256 | bytes 21499904 | tf_op jit(solution)/shard_map/nk,nd->kd/dot_general | solution.py:32
  197.0 0.0 all-reduce.6.cloned.1.call-update
  197.1 0.0 reduce-scatter.2.cloned.1.call-start
  197.1 8.0 %fusion.2 = f32[4096]{0:T(1024)S(1)} fusion(f32[4096,1024]{1,0:T(8,128)} %get-tuple-element.15, f32[1024]{0:T(1024)S(1)} %log_add_fusion.1), kind=kLoop, calls=%fused_computation.11 | loop fusion | flops 8384512 | bytes 16797696 | tf_op jit(solution)/shard_map/reduce_sum | solution.py:31
  205.2 14.3 %psum.53 = f32[4096]{0:T(1024)S(1)} all-reduce(f32[4096]{0:T(1024)S(1)} %fusion.2), channel_id=1, replica_groups=mesh['fit'=2,'comp'=4,'data'=4] {'data'}, use_global_device_ids=true, to_apply=%region_14.0 | all-reduce | flops 4096 | bytes 32768 | tf_op jit(solution)/shard_map/psum | solution.py:34
  219.5 65.9 %all-reduce.6.cloned.1.call-done = f32[4096,256]{1,0:T(8,128)} async-done(((f32[4096,256]{1,0:T(8,128)}), f32[4096,256]{1,0:T(8,128)}) %all-reduce.6.cloned.1.call-update) | async-done | bytes 4194320 | tf_op jit(solution)/shard_map/psum | solution.py:34
  285.4 2.9 multiply_reduce_fusion
  288.3 10.7 %fusion.22 = (f32[1024]{0:T(1024)S(1)}, f32[4096,1024]{1,0:T(8,128)}) fusion(f32[4096]{0:T(1024)S(1)} %multiply_reduce_fusion, bf16[1024,256]{1,0:T(8,128)(2,1)S(1)} %copy-done, f32[4096,256]{1,0:T(8,128)} %all-reduce.6.cloned.1.call-done, f32[4096]{0:T(1024)S(1)} %get-tuple-element.5, f32[1024]{0:T(1024)S(1)} %fusion.18, f32[]{:T(128)} %bitcast.2, ...), kind=kOutput, calls=%fused_computation.44 | convolution fusion | flops 2174745600 | bytes 21553156 | tf_op jit(solution)/shard_map/nd,kd->nk/dot_general | solution.py:24
  299.0 9.6 %pmax.23 = f32[1024]{0:T(1024)S(1)} all-reduce(f32[1024]{0:T(1024)S(1)} %get-tuple-element.16), channel_id=1, replica_groups=mesh['fit'=2,'comp'=4,'data'=4] {'comp'}, use_global_device_ids=true, to_apply=%region_18.0 | all-reduce | flops 1024 | bytes 8192 | tf_op jit(solution)/shard_map/pmax | solution.py:27
  308.6 8.0 %exponential_reduce_fusion = f32[1024]{0:T(1024)S(1)} fusion(f32[4096,1024]{1,0:T(8,128)} %get-tuple-element.17, f32[1024]{0:T(1024)S(1)} %pmax.23), kind=kLoop, calls=%fused_computation | loop fusion | flops 8387584 | bytes 16785408 | tf_op jit(solution)/shard_map/reduce_sum | solution.py:28
  316.7 6.6 %psum.55 = f32[1024]{0:T(1024)S(1)} all-reduce(f32[1024]{0:T(1024)S(1)} %exponential_reduce_fusion), channel_id=1, replica_groups=mesh['fit'=2,'comp'=4,'data'=4] {'comp'}, use_global_device_ids=true, to_apply=%region_20.0 | all-reduce | flops 1024 | bytes 8192 | tf_op jit(solution)/shard_map/psum | solution.py:28
  323.3 0.0 copy-start.1
  323.3 0.0 copy-start.2
  323.3 10.3 %fusion.6 = f32[4096,256]{1,0:T(8,128)} fusion(bf16[1024,256]{1,0:T(8,128)(2,1)S(1)} %copy-done, f32[4096,1024]{1,0:T(8,128)} %get-tuple-element.17, f32[1024]{0:T(1024)S(1)} %log_add_fusion), kind=kOutput, calls=%fused_computation.15 | convolution fusion | flops 2155872256 | bytes 21499904 | tf_op jit(solution)/shard_map/nk,nd->kd/dot_general | solution.py:32
  333.6 0.0 reduce-scatter.2.cloned.1.call-update
  333.6 0.0 copy-done.2
  333.6 0.6 dynamic-slice
  334.9 0.0 copy-done.1
  334.9 8.1 %fusion.4 = f32[4096]{0:T(1024)S(1)} fusion(f32[4096,1024]{1,0:T(8,128)} %get-tuple-element.17, f32[1024]{0:T(1024)S(1)} %log_add_fusion), kind=kLoop, calls=%fused_computation.13 | loop fusion | flops 8384512 | bytes 16797696 | tf_op jit(solution)/shard_map/reduce_sum | solution.py:31
  343.0 13.0 %all-reduce = f32[4096]{0:T(1024)S(1)} all-reduce(f32[4096]{0:T(1024)S(1)} %fusion.4), channel_id=3, replica_groups=mesh['fit'=2,'comp'=4,'data'=4] {'data'}, use_global_device_ids=true, to_apply=%region_23.0.clone | all-reduce | flops 4096 | bytes 32768
  356.0 0.6 multiply_log_fusion.2
  356.6 23.8 %reduce-scatter.2.cloned.1.call-done = f32[1024,256]{1,0:T(8,128)} async-done(((f32[4096,256]{1,0:T(8,128)}), f32[1024,256]{1,0:T(8,128)}) %reduce-scatter.2.cloned.1.call-update) | async-done | bytes 1048592 | tf_op jit(solution)/shard_map/reduce_scatter | solution.py:36
  380.4 2.4 broadcast_divide_fusion.4
  (5 shorter events, 0.0 us)
Async XLA Ops:
  7.2 141.7 %all-reduce.4.cloned.1.call-start = ((), (), s32[]{:S(2)}) async-start(), calls=%async_computation.1 | async-start | bytes 8388608 | tf_op jit(solution)/shard_map/psum | solution.py:34
  12.6 36.4 %copy-start = (bf16[1024,256]{1,0:T(8,128)(2,1)S(1)}, bf16[1024,256]{1,0:T(8,128)(2,1)}, u32[]{:S(2)}) copy-start(bf16[1024,256]{1,0:T(8,128)(2,1)} %param.4) | copy-start | bytes 1572868
  60.1 225.4 %all-reduce.6.cloned.1.call-start = ((), (), s32[]{:S(2)}) async-start(), calls=%async_computation.2 | async-start | bytes 8388608 | tf_op jit(solution)/shard_map/psum | solution.py:34
  197.1 183.4 %reduce-scatter.2.cloned.1.call-start = ((), (), s32[]{:S(2)}) async-start(), calls=%async_computation.3 | async-start | bytes 5242880 | tf_op jit(solution)/shard_map/reduce_scatter | solution.py:36
  323.3 11.6 %copy-start.1 = (f32[1024]{0:T(1024)}, f32[1024]{0:T(1024)S(1)}, u32[]{:S(2)}) copy-start(f32[1024]{0:T(1024)S(1)} %log_add_fusion) | copy-start | bytes 12292
  323.3 10.3 %copy-start.2 = (u32[32]{0:T(128)S(1)}, u32[32]{0:T(128)}, u32[]{:S(2)}) copy-start(u32[32]{0:T(128)} %constant.21) | copy-start | bytes 388
Sparse Core Ops, SparseCore 0:
  60.2 88.6 all-reduce.3
  197.2 88.1 all-reduce.5
  333.8 46.6 reduce-scatter.1
where the time goes:
time: 391 us; the launch traced here: 389 us
  waiting for transfers between devices  156 us (40%)
  blocking collectives  92 us (24%)
  matrix products  63.9 us (16%)
  other arithmetic  61.3 us (16%)
  between operations  14.5 us (4%)
    psum x2, waiting for transfers between devices, local_fit(): stat_sum, counts = lax.psum((stat_part, count_part), 'data')  132 us
    dot_general x3, matrix products, local_fit(): jnp.einsum('nd,kd->nk', points, mu_bf, preferred_element_type=jnp.float32)  32.3 us
    dot_general x3, matrix products, local_fit(): jnp.einsum('nk,nd->kd', respons.astype(jnp.bfloat16), points, preferred_e...  31.6 us
    pmax x3, blocking collectives, local_fit(): row_max = lax.pmax(jnp.max(logits, axis=1), 'comp')  30 us
    psum x2, blocking collectives, local_fit(): stat_sum, counts = lax.psum((stat_part, count_part), 'data')  29 us
    reduce_sum x3, other arithmetic, local_fit(): count_part = jnp.sum(respons, axis=0)  24.4 us
    reduce_sum x3, other arithmetic, local_fit(): jnp.sum(jnp.exp(logits - row_max[:, None]), axis=1)  24.1 us
    reduce_scatter x1, waiting for transfers between devices, local_fit(): lax.psum_scatter(stat_part, 'data', scatter_dimension=0, tiled=True)  23.8 us
  transfers between devices with their start and end apart: 3, of which 3 were waited for; matrix products, arithmetic and copies ran while one was open for 7% of the time, Pallas kernels for 0%

commit v1 on v0

v1 whole, which is shorter than its diff:
```python
import functools
import math

import jax
import jax.numpy as jnp
from jax import lax
from jax.experimental import pallas as pl
from jax.experimental.pallas import tpu as pltpu
from jax.sharding import PartitionSpec as P

MEAN_EPS = 1e-6
PRIOR_ALPHA = 1e-3
LOG2E = math.log2(math.e)
LN2 = math.log(2.0)
F32 = jnp.float32
BF16 = jnp.bfloat16
MESH = pl.DeviceIdType.MESH
NT = (((1,), (1,)), ((), ()))
T = 256
RB = 64


def em_kernel(
    n_sweeps, n_total,
    beta_ref, x_hbm, mu_hbm, lp_hbm,
    out_mu, out_lp, out_lse,
    x_all, mu_f, lp_v, mu_bf, cvec, eb, mb, sb0, sb1, lam, lam_all, s1_buf, s2_buf, nacc, rbuf, s_acc,
    loc_sem, xs_send, xs_recv, s1_send, s1_recv, s2_send, s2_recv,
):
    n_pts = x_all.shape[0]
    n_loc = x_hbm.shape[0]
    k_loc = mu_f.shape[0]
    n_tiles = n_pts // T
    tiles_blk = n_loc // T
    nb = k_loc // RB
    rows_blk = n_loc // 128
    half_rows = lam.shape[1]
    f_i, z_i, d_i = lax.axis_index("fit"), lax.axis_index("comp"), lax.axis_index("data")
    nz, nd = 4, 4
    sib = d_i + 1 - 2 * lax.rem(d_i, 2)
    ypeer = lax.rem(d_i + 2, nd)
    cross = lax.rem(sib + 2, nd)
    quad = [sib, ypeer, cross]
    zs = [lax.rem(z_i + k, nz) for k in (1, 2, 3)]

    def dev(z, d):
        return (f_i, z, d)

    def rcopy(src, dst, ssem, rsem, device):
        return pltpu.make_async_remote_copy(
            src_ref=src, dst_ref=dst, send_sem=ssem, recv_sem=rsem, device_id=device, device_id_type=MESH
        )

    barrier = pltpu.get_barrier_semaphore()
    for q in quad:
        pl.semaphore_signal(barrier, inc=1, device_id=dev(z_i, q), device_id_type=MESH)
    for z in zs:
        pl.semaphore_signal(barrier, inc=1, device_id=dev(z, d_i), device_id_type=MESH)

    def blk_rows(b):
        return pl.ds(pl.multiple_of(b * n_loc, n_loc), n_loc)

    cp_x = pltpu.make_async_copy(x_hbm, x_all.at[blk_rows(d_i), :], loc_sem.at[0])
    cp_mu = pltpu.make_async_copy(mu_hbm.at[pl.ds(pl.multiple_of(d_i * k_loc, k_loc), k_loc), :], mu_f, loc_sem.at[1])
    cp_lp = pltpu.make_async_copy(lp_hbm.at[pl.ds(pl.multiple_of(d_i * rows_blk, rows_blk), rows_blk), :], lp_v, loc_sem.at[2])
    cp_x.start()
    cp_mu.start()
    cp_lp.start()
    cp_x.wait()
    pl.semaphore_wait(barrier, 6)
    x_sib = rcopy(x_all.at[blk_rows(d_i), :], x_all.at[blk_rows(d_i), :], xs_send.at[0], xs_recv.at[0], dev(z_i, sib))
    x_sib.start()

    def piece(b, p):
        return x_all.at[pl.ds(pl.multiple_of(b * n_loc + p * T, T), T), :]

    x_y = []
    for p in range(tiles_blk):
        c = rcopy(piece(d_i, p), piece(d_i, p), xs_send.at[1 + p], xs_recv.at[1 + p], dev(z_i, ypeer))
        c.start()
        x_y.append(c)
    cp_mu.wait()
    cp_lp.wait()

    eye = lax.broadcasted_iota(jnp.int32, (128, 128), 0) == lax.broadcasted_iota(jnp.int32, (128, 128), 1)

    bp0 = beta_ref[0] * LOG2E
    for g in range(k_loc // 128):
        r = slice(g * 128, (g + 1) * 128)
        m = mu_f[r, :]
        mu_bf[r, :] = m.astype(BF16)
        sq = m * m
        w = jnp.where(eye, lp_v[g : g + 1, :] * LOG2E, 0.0) - bp0 * (sq[:, :128] + sq[:, 128:])
        cvec[r, :] = jnp.broadcast_to(jnp.sum(w, axis=1, keepdims=True), (128, 128))

    def e_pair(tiles, b2):
        sbs = (sb0, sb1)
        logits = []
        for q in range(2):
            xt = x_all[pl.ds(pl.multiple_of(tiles[q] * T, T), T), :]
            logits.append(lax.dot_general(mu_bf[...], xt, NT, preferred_element_type=F32))
        for j in range(nb):
            r = slice(j * RB, (j + 1) * RB)
            for q in range(2):
                cc = cvec[r, :]
                l3 = (logits[q][r] * b2 + jnp.concatenate([cc, cc], axis=1)).reshape(RB // 8, 8, T)
                m = jnp.max(l3, axis=0)
                e = jnp.exp2(l3 - m[None])
                eb[tiles[q], r, :] = e.reshape(RB, T)
                mb[tiles[q], j] = m
                sbs[q][j] = jnp.sum(e, axis=0)
        for q in range(2):
            t = tiles[q]
            mx = mb[t, 0]
            for j in range(1, nb):
                mx = jnp.maximum(mx, mb[t, j])
            mx = jnp.max(mx, axis=0, keepdims=True)
            s = sbs[q][0] * jnp.exp2(mb[t, 0] - mx)
            for j in range(1, nb):
                s = s + sbs[q][j] * jnp.exp2(mb[t, j] - mx)
            lm = mx + jnp.log2(jnp.sum(s, axis=0, keepdims=True))
            per_half = n_tiles // 2
            h = t // per_half
            tl = lax.rem(t, per_half)
            lam[h, pl.ds(2 * tl, 1), :] = lm[:, :128]
            lam[h, pl.ds(2 * tl + 1, 1), :] = lm[:, 128:]

    def s1_start(s, h):
        cs = []
        for k, q in enumerate(quad):
            c = rcopy(lam.at[h], s1_buf.at[s, h, d_i], s1_send.at[s, h, k], s1_recv.at[s, h, d_i], dev(z_i, q))
            c.start()
            cs.append(c)
        return cs

    def lse4(vals):
        mx = functools.reduce(jnp.maximum, vals)
        tot = functools.reduce(lambda a, b: a + b, [jnp.exp2(v - mx) for v in vals])
        return mx + jnp.log2(tot)

    def s1_finish(s, h):
        for q in quad:
            rcopy(lam.at[h], s1_buf.at[s, h, q], s1_send.at[s, h, 0], s1_recv.at[s, h, q], dev(z_i, q)).wait_recv()
        v = lse4([lam[h]] + [s1_buf[s, h, q] for q in quad])
        s2_buf[s, h, z_i] = v

    def s2_start(s, h):
        cs = []
        for k, z in enumerate(zs):
            c = rcopy(s2_buf.at[s, h, z_i], s2_buf.at[s, h, z_i], s2_send.at[s, h, k], s2_recv.at[s, h, z_i], dev(z, d_i))
            c.start()
            cs.append(c)
        return cs

    def s2_finish(s, h):
        for z in zs:
            rcopy(s2_buf.at[s, h, z], s2_buf.at[s, h, z], s2_send.at[s, h, 0], s2_recv.at[s, h, z], dev(z, d_i)).wait_recv()
        lam_all[h * half_rows : (h + 1) * half_rows, :] = lse4([s2_buf[s, h, z] for z in range(nz)])

    def m_half(h):
        per_chunk = rbuf.shape[1] // T

        def chunk(i, _):
            t0 = h * (n_tiles // 2) + i * per_chunk
            for k in range(per_chunk):
                t = t0 + k
                lrow = jnp.concatenate([lam_all[pl.ds(2 * t, 1), :], lam_all[pl.ds(2 * t + 1, 1), :]], axis=1)
                for b in range(nb):
                    r = slice(b * RB, (b + 1) * RB)
                    fac = jnp.exp2(mb[t, b] - lrow)
                    rv = (eb[t, r, :].reshape(RB // 8, 8, T) * fac[None]).reshape(RB, T)
                    nacc[r, :] += rv[:, :128] + rv[:, 128:]
                    rbuf[r, k * T : (k + 1) * T] = rv.astype(BF16)
            xt = x_all[pl.ds(pl.multiple_of(t0 * T, T), per_chunk * T), :]
            s_acc[...] += jnp.dot(rbuf[...], xt, preferred_element_type=F32)
            return 0

        lax.fori_loop(0, n_tiles // 2 // per_chunk, chunk, 0)

    def update(s):
        last = s + 1 == n_sweeps
        inv_tot = 1.0 / (n_pts + n_total * PRIOR_ALPHA)
        if not last:
            bp = beta_ref[s + 1] * LOG2E
        for b in range(nb):
            r = slice(b * RB, (b + 1) * RB)
            st = s_acc[r, :]
            n = jnp.sum(nacc[r, :], axis=1, keepdims=True)
            mu = st * (1.0 / (n + MEAN_EPS))
            l2 = jnp.log2((n + PRIOR_ALPHA) * inv_tot)
            if last:
                out_mu[r, :] = mu
                cvec[r, :] = jnp.broadcast_to(l2 * LN2, (RB, 128))
            else:
                mu_bf[r, :] = mu.astype(BF16)
                sq = mu * mu
                p = jnp.sum(sq[:, :128] + sq[:, 128:], axis=1, keepdims=True)
                cvec[r, :] = jnp.broadcast_to(l2 - bp * p, (RB, 128))
        if last:
            for g in range(k_loc // 128):
                out_lp[g : g + 1, :] = jnp.sum(jnp.where(eye, cvec[g * 128 : (g + 1) * 128, :], 0.0), axis=0, keepdims=True)

    for s in range(n_sweeps):
        b2 = beta_ref[s] * (2.0 * LOG2E)
        nacc[...] = jnp.zeros_like(nacc)
        s_acc[...] = jnp.zeros_like(s_acc)
        sends = []
        if s == 0:
            def own(i, _):
                t = d_i * tiles_blk + 2 * i
                e_pair((t, t + 1), b2)
                return 0

            lax.fori_loop(0, tiles_blk // 2, own, 0)
            rcopy(x_all.at[blk_rows(sib), :], x_all.at[blk_rows(sib), :], xs_send.at[0], xs_recv.at[0], dev(z_i, sib)).wait_recv()

            def sibl(i, _):
                t = sib * tiles_blk + 2 * i
                e_pair((t, t + 1), b2)
                return 0

            lax.fori_loop(0, tiles_blk // 2, sibl, 0)
            fwd = []

            def take(p):
                rcopy(piece(ypeer, p), piece(ypeer, p), xs_send.at[1 + p], xs_recv.at[1 + p], dev(z_i, ypeer)).wait_recv()
                c = rcopy(piece(ypeer, p), piece(ypeer, p), xs_send.at[1 + tiles_blk + p], xs_recv.at[1 + tiles_blk + p], dev(z_i, sib))
                c.start()
                fwd.append(c)

            take(0)
            for p in range(tiles_blk):
                if p + 1 < tiles_blk:
                    take(p + 1)
                rcopy(piece(cross, p), piece(cross, p), xs_send.at[1 + tiles_blk + p], xs_recv.at[1 + tiles_blk + p], dev(z_i, sib)).wait_recv()
                e_pair((ypeer * tiles_blk + p, cross * tiles_blk + p), b2)
            sends += s1_start(s, 0) + s1_start(s, 1)
            x_sib.wait_send()
            for c in x_y + fwd:
                c.wait_send()
            s1_finish(s, 0)
            sends += s2_start(s, 0)
            s1_finish(s, 1)
            sends += s2_start(s, 1)
        else:
            for h in range(2):
                def body(i, _, h=h):
                    t = h * (n_tiles // 2) + 2 * i
                    e_pair((t, t + 1), b2)
                    return 0

                lax.fori_loop(0, n_tiles // 4, body, 0)
                sends += s1_start(s, h)
            for h in range(2):
                s1_finish(s, h)
                sends += s2_start(s, h)
        if s + 1 == n_sweeps:
            for g in range(rows_blk):
                xf = x_all[pl.ds(pl.multiple_of(d_i * n_loc + g * 128, 128), 128), :].astype(F32)
                sq = xf * xf
                qc = jnp.sum(sq[:, :128] + sq[:, 128:], axis=1, keepdims=True)
                lp_v[g : g + 1, :] = jnp.sum(jnp.where(eye, qc, 0.0), axis=0, keepdims=True)
        for h in range(2):
            s2_finish(s, h)
            m_half(h)
        for c in sends:
            c.wait_send()
        update(s)
    out_lse[...] = lam_all[pl.ds(pl.multiple_of(d_i * rows_blk, rows_blk), rows_blk), :] * LN2 - beta_ref[n_sweeps - 1] * lp_v[...]


def solution(mesh):
    n_comp_dev = mesh.shape["comp"]
    n_data_dev = mesh.shape["data"]

    def local_fit(points, mu_init, logpi_init, inv_temp):
        n_loc, dim = points.shape
        k_all = mu_init.shape[0]
        n_pts = n_loc * n_data_dev
        k_loc = k_all // n_data_dev
        n_total = k_all * n_comp_dev
        n_sweeps = inv_temp.shape[0]
        n_tiles = n_pts // T
        nb = k_loc // RB
        half_rows = n_pts // 256
        dma = pltpu.SemaphoreType.DMA
        vmem = pl.BlockSpec(memory_space=pltpu.VMEM)
        hbm = pl.BlockSpec(memory_space=pl.ANY)
        tiles_blk = n_loc // T
        means, log_pi, log_norm = pl.pallas_call(
            functools.partial(em_kernel, n_sweeps, n_total),
            out_shape=(
                jax.ShapeDtypeStruct((k_loc, dim), F32),
                jax.ShapeDtypeStruct((k_loc // 128, 128), F32),
                jax.ShapeDtypeStruct((n_loc // 128, 128), F32),
            ),
            in_specs=[pl.BlockSpec(memory_space=pltpu.SMEM), hbm, hbm, hbm],
            out_specs=(vmem, vmem, vmem),
            scratch_shapes=[
                pltpu.VMEM((n_pts, dim), BF16),
                pltpu.VMEM((k_loc, dim), F32),
                pltpu.VMEM((k_loc // 128, 128), F32),
                pltpu.VMEM((k_loc, dim), BF16),
                pltpu.VMEM((k_loc, 128), F32),
                pltpu.VMEM((n_tiles, k_loc, T), F32),
                pltpu.VMEM((n_tiles, nb, 8, T), F32),
                pltpu.VMEM((nb, 8, T), F32),
                pltpu.VMEM((nb, 8, T), F32),
                pltpu.VMEM((2, half_rows, 128), F32),
                pltpu.VMEM((2 * half_rows, 128), F32),
                pltpu.VMEM((n_sweeps, 2, 4, half_rows, 128), F32),
                pltpu.VMEM((n_sweeps, 2, 4, half_rows, 128), F32),
                pltpu.VMEM((k_loc, 128), F32),
                pltpu.VMEM((k_loc, min(n_pts // 2, 4 * T)), BF16),
                pltpu.VMEM((k_loc, dim), F32),
                dma((3,)),
                dma((1 + 2 * tiles_blk,)),
                dma((1 + 2 * tiles_blk,)),
                dma((n_sweeps, 2, 3)),
                dma((n_sweeps, 2, 4)),
                dma((n_sweeps, 2, 3)),
                dma((n_sweeps, 2, 4)),
            ],
            compiler_params=pltpu.CompilerParams(
                collective_id=0, has_side_effects=True, vmem_limit_bytes=60 * 2**20
            ),
            name="em_sweeps",
        )(inv_temp, points, mu_init, logpi_init.reshape(k_all // 128, 128))
        return means, log_pi.reshape(k_loc), log_norm.reshape(n_loc)

    return jax.shard_map(
        local_fit,
        mesh=mesh,
        in_specs=(P(("fit", "data"), None), P(("fit", "comp"), None), P(("fit", "comp")), P(None)),
        out_specs=(P(("fit", "comp", "data"), None), P(("fit", "comp", "data")), P(("fit", "data"))),
        check_vma=False,
    )
```

time: 391 us -> 66.9 us (0.17)
  the two profiles are of different devices: /device:TPU:1 before, /device:TPU:0 now
where the time goes in v1:
time: 66.9 us; the launch traced here: 66.7 us
  Pallas kernels  61.3 us (92%)
  local copies, waits for them, and re-layouts  4.8 us (7%)
    pallas_call x1, Pallas kernels, local_fit(): pl.pallas_call(functools.partial(em_kernel, n_sweeps, n_total), out_shape...  61.3 us
    unnamed x3, local copies, waits for them, and re-layouts  4.8 us

profile of v1, /device:TPU:0, one launch (start us, length us, event | category | flops | bytes accessed | tf_op | source)
XLA Modules:
  0.0 66.7 jit_solution(3907700286106388648)
XLA Ops:
  0.6 61.3 %em_sweeps.1 = (f32[1024,256]{1,0:T(8,128)}, f32[8,128]{1,0:T(8,128)}, f32[8,128]{1,0:T(8,128)}) custom-call(f32[3]{0:T(128)} %beta_ref.1, bf16[1024,256]{1,0:T(8,128)(2,1)} %x_hbm.1, f32[4096,256]{1,0:T(8,128)} %mu_hbm.1, f32[32,128]{1,0:T(8,128)} %bitcast.3), custom_call_target="tpu_custom_call" | custom-call | tf_op jit(solution)/shard_map/em_sweeps/pallas_call | solution.py:290
  61.9 2.3 %copy.10 = f32[1024,256]{1,0:T(8,128)} copy(f32[1024,256]{1,0:T(8,128)} %get-tuple-element.12) | data formatting | bytes 2097152
  64.2 1.3 %copy.11 = f32[1024]{0:T(1024)} copy(f32[1024]{0:T(1024)} %bitcast.5) | data formatting | bytes 8192
  65.4 1.3 %copy.12 = f32[1024]{0:T(1024)} copy(f32[1024]{0:T(1024)} %bitcast.4) | data formatting | bytes 8192
